TPU v7x, 32 devices: a whole 2x2x4 slice. The times are simulated.
32 devices in a mesh: row: 4 (over x, core), col: 8 (over z, y).
Axes of the slice: x: 2, y: 2, z: 4, core: 2. Of those that a mesh axis runs over, the one named last changes fastest.
Arguments:
- hamiltonian: bfloat16 [2912, 2912], P('row', 'col'), may hold values from -6 to 6
- new_atom: int32 [224], replicated, may hold values from 0 to 223, as said below
- pattern: int32 [224, 224], P('row', 'col'), may hold values 0 or 1
Outputs:
- sign_matrix: float32 [2912, 2912], P('row', 'col')
Inputs may be any that keep to these rules, and one draw needn't show every extreme that they name: `new_atom`: each old atom appears once. Block column b holds atoms b * 28 to (b + 1) * 28 - 1 in both orders. For each new block column d and each v from 0 to 27, exactly one atom of new block column d comes from old block column (d - 1 - (v mod 8)) mod 8, so the number of atoms that old block column b sends to new block column (b + k) mod 8 is the number of such v with (1 + v) mod 8 = k.
All inputs are finite; a program needn't handle non-finite values. No bound on the sum of `pattern` on one device may be relied on, other than what follows from the above.
Results may differ from a plain program's by a relative error of at most 0.0029.
Values may be sent and summed in bfloat16 or wider, within the bound.
A program may use at most 64 MiB of HBM per device.

v0:
```python
import jax
import jax.numpy as jnp
from jax import lax
from jax.sharding import PartitionSpec as P

NBF = 13
BF = jnp.bfloat16
F32 = jnp.float32


def mm(a, b):
    return jnp.dot(a, b, preferred_element_type=F32)


def spread(n):
    i = lax.broadcasted_iota(jnp.int32, (n * NBF, n), 0)
    a = lax.broadcasted_iota(jnp.int32, (n * NBF, n), 1) * NBF
    return (i >= a) & (i < a + NBF)


def on_device(hamiltonian, new_atom, pattern):
    rows_here, cols_here = hamiltonian.shape
    order = rows_here * lax.axis_size("row")
    atoms = order // NBF
    ar, ac = pattern.shape
    row_here = lax.axis_index("row")
    col_here = lax.axis_index("col")
    panel = lax.all_gather(hamiltonian, "col", axis=1, tiled=True)
    pat = lax.all_gather(pattern.astype(BF), ("row", "col"), axis=0, tiled=False)
    n_row, n_col = (lax.axis_size("row"), lax.axis_size("col"))
    pat = pat.reshape(n_row, n_col, ar, ac).transpose(0, 2, 1, 3).reshape(atoms, atoms)
    old = jnp.arange(atoms, dtype=jnp.int32)
    perm = (new_atom[:, None] == old[None, :]).astype(BF)
    mine = (new_atom[None, :] == row_here * ar + jnp.arange(ar, dtype=jnp.int32)[:, None]).astype(
        BF
    )
    pat_rows = mm(mine, pat).astype(BF)
    e_row = spread(ar)
    e_col = spread(ac)
    e_rowb = e_row.astype(BF)
    rows_masked = mm(e_rowb, mm(pat_rows, perm).astype(BF)).astype(BF)
    keep = mm(rows_masked, spread(atoms).astype(BF).T).astype(BF)
    m = panel * keep
    total = lax.psum(jnp.sum(m.astype(F32) ** 2), "row")
    s = lax.rsqrt(total / order)

    def old_index(n, here, e):
        mine_atoms = lax.dynamic_slice_in_dim(new_atom, here * n, n)
        base = jnp.sum(
            jnp.where(e, (mine_atoms - jnp.arange(n, dtype=jnp.int32))[None, :], 0), axis=1
        )
        return base * NBF + jnp.arange(n * NBF, dtype=jnp.int32)

    full = jnp.arange(order, dtype=jnp.int32)
    pick_col = (full[:, None] == old_index(ac, col_here, e_col)[None, :]).astype(BF)
    pick_row = (old_index(ar, row_here, e_row)[:, None] == full[None, :]).astype(BF)
    right = lax.all_gather(mm(m, pick_col).astype(BF), "row", axis=0, tiled=True)
    e_colt = e_col.astype(BF).T
    here_cols = lax.dynamic_slice_in_dim(pat_rows, col_here * ac, ac, axis=1)
    keep_sq = mm(mm(e_rowb, here_cols).astype(BF), e_colt)
    square = (mm(m, right) * (s * s) * keep_sq).astype(BF)
    square = lax.all_gather(square, "row", axis=0, tiled=True)
    cube = lax.all_gather((mm(m, square) * s).astype(BF), "row", axis=0, tiled=True)
    start = (mm(pick_row, right) * s).astype(BF).astype(F32)
    keep_out = mm(mm(e_rowb, pattern.astype(BF)).astype(BF), e_colt)
    return keep_out * (1.5 * start - 0.5 * mm(pick_row, cube))


def solution(mesh):
    in_specs = (P("row", "col"), P(), P("row", "col"))
    out_specs = P("row", "col")
    return jax.shard_map(
        on_device, mesh=mesh, in_specs=in_specs, out_specs=out_specs, check_vma=False
    )
```

profile of v0, /device:TPU:0, one launch (start us, length us, event | category | flops | bytes accessed | tf_op | source)
XLA Modules:
  0.0 211.8 jit_solution(7994260219636314159)
XLA Ops:
  6.5 0.0 all-gather.14.cloned.1.call-start
  6.5 0.7 all-gather.14.cloned.1.call-update
  7.3 0.0 all-gather.8.cloned.1.call-start
  7.3 0.7 convert_bitcast_fusion
  8.0 75.1 %all-gather.2 = bf16[32,56,28]{1,2,0:T(8,128)(2,1)S(1)} all-gather(bf16[1,56,28]{1,2,0:T(8,128)(2,1)S(1)} %convert_bitcast_fusion), channel_id=2, replica_groups=mesh['row'=4,'col'=8] {'row','col'}, dimensions={0}, use_global_device_ids=true | all-gather | bytes 103488 | tf_op jit(solution)/shard_map/all_gather | solution.py:29
  83.2 0.2 copy.12
  83.3 0.2 reshape.30
  83.5 0.8 iota_subtract_fusion
  84.3 0.1 select_reduce_fusion.1
  84.4 0.9 convolution_convert_fusion.5
  85.3 0.9 convolution_convert_fusion.4
  86.2 5.0 %all-gather.14.cloned.1.call-done = bf16[8,364,728]{1,2,0:T(8,128)(2,1)} async-done(((bf16[1,364,728]{1,2,0:T(8,128)(2,1)}), bf16[8,364,728]{1,2,0:T(8,128)(2,1)}) %all-gather.14.cloned.1.call-update) | async-done | bytes 4239888 | tf_op jit(solution)/shard_map/all_gather | solution.py:28
  91.2 4.9 %copy.9 = bf16[8,364,728]{1,0,2:T(8,128)(2,1)} copy(bf16[8,364,728]{1,2,0:T(8,128)(2,1)} %all-gather.14.cloned.1.call-done) | data formatting | bytes 8479744 | tf_op jit(solution)/shard_map/all_gather | solution.py:28
  96.1 8.6 %reshape.34 = bf16[2912,728]{0,1:T(8,128)(2,1)} reshape(bf16[8,364,728]{1,0,2:T(8,128)(2,1)} %copy.9) | data formatting | bytes 8479744
  104.7 6.9 %multiply_reduce_fusion = (f32[]{:T(128)}, bf16[728,2912]{1,0:T(8,128)(2,1)}) fusion(s32[224]{0:T(256)S(1)} %get-tuple-element.8, s32[224]{0:T(256)S(1)} %get-tuple-element.7, bf16[56,224]{1,0:T(8,128)(2,1)S(1)} %convolution_convert_fusion.4, s32[56]{0:T(128)S(1)} %get-tuple-element.10, s32[56]{0:T(128)S(1)} %get-tuple-element.9, bf16[2912,728]{0,1:T(8,128)(2,1)} %reshape.34), kind=kOutput, calls=%fused_computation | convolution fusion | flops 987197120 | bytes 8507076 | tf_op jit(solution)/shard_map/dot_general | solution.py:12
  111.6 5.5 %fusion.19 = bf16[728,364]{1,0:T(8,128)(2,1)} fusion(bf16[728,2912]{1,0:T(8,128)(2,1)} %get-tuple-element.6, s32[364]{0:T(512)S(1)} %iota_add_fusion.1), kind=kOutput, calls=%fused_computation.28 | convolution fusion | flops 1544638336 | bytes 4771312 | tf_op jit(solution)/shard_map/dot_general | solution.py:12
  117.1 0.0 all-gather.8.cloned.1.call-update
  117.1 0.0 all-gather.10.cloned.1.call-start
  117.2 6.2 %psum.7 = f32[]{:T(128)} all-reduce(f32[]{:T(128)} %get-tuple-element.5), channel_id=1, replica_groups=mesh['row'=4,'col'=8] {'row'}, use_global_device_ids=true, to_apply=%region_3.4 | all-reduce | flops 1 | bytes 8 | tf_op jit(solution)/shard_map/psum | solution.py:44
  124.2 15.2 %all-gather.8.cloned.1.call-done = bf16[2912,364]{1,0:T(8,128)(2,1)} async-done(((bf16[728,364]{1,0:T(8,128)(2,1)}), bf16[2912,364]{1,0:T(8,128)(2,1)}) %all-gather.8.cloned.1.call-update) | async-done | bytes 2119952 | tf_op jit(solution)/shard_map/all_gather | solution.py:57
  139.3 5.4 %convolution_multiply_fusion.1 = f32[728,364]{1,0:T(8,128)S(1)} fusion(bf16[728,2912]{1,0:T(8,128)(2,1)} %get-tuple-element.6, bf16[2912,364]{1,0:T(8,128)(2,1)} %all-gather.8.cloned.1.call-done, f32[]{:T(128)S(6)} %mul.104), kind=kOutput, calls=%fused_computation.17 | convolution fusion | flops 1543578368 | bytes 7419780 | tf_op jit(solution)/shard_map/dot_general | solution.py:12
  144.7 1.5 fusion.17
  146.2 0.0 all-gather.10.cloned.1.call-update
  146.2 0.0 copy-start.1
  146.2 0.0 copy-start.2
  146.2 0.2 all-gather.12.cloned.1.call-start
  146.5 23.3 %all-gather.10.cloned.1.call-done = bf16[2912,364]{1,0:T(8,128)(2,1)} async-done(((bf16[728,364]{1,0:T(8,128)(2,1)}), bf16[2912,364]{1,0:T(8,128)(2,1)}) %all-gather.10.cloned.1.call-update) | async-done | bytes 2119952 | tf_op jit(solution)/shard_map/all_gather | solution.py:62
  169.7 6.2 %fusion.18 = bf16[728,364]{1,0:T(8,128)(2,1)} fusion(bf16[728,2912]{1,0:T(8,128)(2,1)} %get-tuple-element.6, bf16[2912,364]{1,0:T(8,128)(2,1)} %all-gather.10.cloned.1.call-done, f32[]{:T(128)S(6)} %rsqrt.3), kind=kOutput, calls=%fused_computation.27 | convolution fusion | flops 1543843328 | bytes 6889796 | tf_op jit(solution)/shard_map/dot_general | solution.py:12
  175.9 0.0 all-gather.12.cloned.1.call-update
  176.0 0.0 copy-done.1
  176.0 0.1 iota_subtract_fusion.1
  176.1 0.1 select_reduce_fusion
  176.2 0.0 copy-done.2
  176.2 2.5 %fusion.16 = f32[728,364]{1,0:T(8,128)S(1)} fusion(bf16[2912,364]{1,0:T(8,128)(2,1)S(1)} %copy-done.2, s32[728]{0:T(1024)S(1)} %iota_add_fusion, f32[]{:T(128)S(6)} %rsqrt.3), kind=kOutput, calls=%fused_computation.25 | convolution fusion | flops 1546493184 | bytes 3182820 | tf_op jit(solution)/shard_map/dot_general | solution.py:12
  178.7 0.0 copy-start
  178.7 20.7 %all-gather.12.cloned.1.call-done = bf16[2912,364]{1,0:T(8,128)(2,1)} async-done(((bf16[728,364]{1,0:T(8,128)(2,1)}), bf16[2912,364]{1,0:T(8,128)(2,1)}) %all-gather.12.cloned.1.call-update) | async-done | bytes 2119952 | tf_op jit(solution)/shard_map/all_gather | solution.py:63
  199.5 4.1 %fusion.13 = f32[728,364]{1,0:T(8,128)S(1)} fusion(f32[728,364]{1,0:T(8,128)S(1)} %fusion.16, bf16[2912,364]{1,0:T(8,128)(2,1)} %all-gather.12.cloned.1.call-done, s32[728]{0:T(1024)S(1)} %iota_add_fusion), kind=kOutput, calls=%fused_computation.22 | convolution fusion | flops 1545963264 | bytes 4242784 | tf_op jit(solution)/shard_map/dot_general | solution.py:12
  203.6 0.0 copy-done
  203.6 1.6 convolution_multiply_fusion.3
  (6 shorter events, 0.0 us)
Async XLA Ops:
  6.5 84.7 %all-gather.14.cloned.1.call-start = ((), (), s32[]{:S(2)}) async-start(), calls=%async_computation.3 | async-start | bytes 5031936 | tf_op jit(solution)/shard_map/all_gather | solution.py:28
  7.3 132.1 %all-gather.8.cloned.1.call-start = ((), (), s32[]{:S(2)}) async-start(), calls=%async_computation | async-start | bytes 2795520 | tf_op jit(solution)/shard_map/all_gather | solution.py:57
  117.1 52.6 %all-gather.10.cloned.1.call-start = ((), (), s32[]{:S(2)}) async-start(), calls=%async_computation.1 | async-start | bytes 2795520 | tf_op jit(solution)/shard_map/all_gather | solution.py:62
  146.2 29.8 %copy-start.1 = (s32[224]{0:T(256)S(1)}, s32[224]{0:T(256)}, u32[]{:S(2)}) copy-start(s32[224]{0:T(256)} %param.4) | copy-start | bytes 2692
  146.2 30.0 %copy-start.2 = (bf16[2912,364]{1,0:T(8,128)(2,1)S(1)}, bf16[2912,364]{1,0:T(8,128)(2,1)}, u32[]{:S(2)}) copy-start(bf16[2912,364]{1,0:T(8,128)(2,1)} %all-gather.8.cloned.1.call-done) | copy-start | bytes 6359812
  146.2 53.2 %all-gather.12.cloned.1.call-start = ((), (), s32[]{:S(2)}) async-start(), calls=%async_computation.2 | async-start | bytes 2795520 | tf_op jit(solution)/shard_map/all_gather | solution.py:63
  178.7 24.9 %copy-start = (s32[56,28]{0,1:T(8,128)S(1)}, s32[56,28]{0,1:T(8,128)}, u32[]{:S(2)}) copy-start(s32[56,28]{0,1:T(8,128)} %param.5) | copy-start | bytes 18820
Sparse Core Ops, SparseCore 0:
  9.5 81.6 all-gather.13
  117.2 22.0 all-gather.7
  146.3 23.3 all-gather.9
  176.1 23.3 all-gather.11
where the time goes:
time: 212 us
  blocking collectives  81.4 us (38%)
  waiting for transfers between devices  64.9 us (31%)
  matrix products  35.5 us (17%)
  between operations  14 us (7%)
  local copies, waits for them, and re-layouts  13.8 us (7%)
    all_gather x1, blocking collectives, on_device(): lax.all_gather(pattern.astype(BF), ('row', 'col'), axis=0, tiled=False)  75.1 us
    dot_general x10, matrix products, mm(): return jnp.dot(a, b, preferred_element_type=F32)  35.5 us
    all_gather x1, waiting for transfers between devices, on_device(): square = lax.all_gather(square, 'row', axis=0, tiled=True)  23.3 us
    all_gather x1, waiting for transfers between devices, on_device(): lax.all_gather((mm(m, square) * s).astype(BF), 'row', axis=0, tiled=True)  20.7 us
    all_gather x1, waiting for transfers between devices, on_device(): lax.all_gather(mm(m, pick_col).astype(BF), 'row', axis=0, tiled=True)  15.2 us
    unnamed x7, local copies, waits for them, and re-layouts  8.62 us
    psum x1, blocking collectives, on_device(): total = lax.psum(jnp.sum(m.astype(F32) ** 2), 'row')  6.25 us
    all_gather x1, waiting for transfers between devices, on_device(): panel = lax.all_gather(hamiltonian, 'col', axis=1, tiled=True)  5 us
  transfers between devices with their start and end apart: 4, of which 4 were waited for; matrix products, arithmetic and copies ran while one was open for 3% of the time, Pallas kernels for 0%

commit v1 on v0

--- a/solution.py
+++ b/solution.py
@@ -59,7 +59,14 @@
     here_cols = lax.dynamic_slice_in_dim(pat_rows, col_here * ac, ac, axis=1)
     keep_sq = mm(mm(e_rowb, here_cols).astype(BF), e_colt)
     square = (mm(m, right) * (s * s) * keep_sq).astype(BF)
-    square = lax.all_gather(square, "row", axis=0, tiled=True)
+    size = lax.axis_size("row")
+    hops = [(i_2, (i_2 + 1) % size) for i_2 in range(size)]
+    parts = [square]
+    for stride in range(1, size):
+        parts = [lax.ppermute(parts[0], "row", hops), *parts]
+    whole = jnp.concatenate(parts, axis=0)
+    shift = (lax.axis_index("row") + 1) * parts[-1].shape[0]
+    square = jnp.roll(whole, shift, axis=0)
     cube = lax.all_gather((mm(m, square) * s).astype(BF), "row", axis=0, tiled=True)
     start = (mm(pick_row, right) * s).astype(BF).astype(F32)
     keep_out = mm(mm(e_rowb, pattern.astype(BF)).astype(BF), e_colt)

time: 212 us -> 215 us (1.014)
  waiting for transfers between devices: 64.9 us -> 68.4 us
    ppermute x0 -> x3, waiting for transfers between devices: none -> 26.7 us  [on_device(): parts = [lax.ppermute(parts[0], 'row', hops), *parts]]
    all_gather x1 -> x0, waiting for transfers between devices: 23.3 us -> none  [on_device(): square = lax.all_gather(square, 'row', axis=0, tiled=True)]
    unnamed x7 -> x14, local copies, waits for them, and re-layouts: 8.62 us -> 9.22 us
  transfers between devices with their start and end apart: 4 -> 6, of which waited for: 4 -> 6; matrix products, arithmetic and copies ran while one was open for 3% -> 3% of each run, Pallas kernels for 0% -> 0%
where the time goes in v1:
time: 215 us
  blocking collectives  81.4 us (38%)
  waiting for transfers between devices  68.4 us (32%)
  matrix products  34.2 us (16%)
  local copies, waits for them, and re-layouts  14.5 us (7%)
  between operations  14 us (7%)
    all_gather x1, blocking collectives, on_device(): lax.all_gather(pattern.astype(BF), ('row', 'col'), axis=0, tiled=False)  75.1 us
    dot_general x10, matrix products, mm(): return jnp.dot(a, b, preferred_element_type=F32)  34.2 us
    ppermute x3, waiting for transfers between devices, on_device(): parts = [lax.ppermute(parts[0], 'row', hops), *parts]  26.7 us
    all_gather x1, waiting for transfers between devices, on_device(): lax.all_gather((mm(m, square) * s).astype(BF), 'row', axis=0, tiled=True)  20.7 us
    all_gather x1, waiting for transfers between devices, on_device(): lax.all_gather(mm(m, pick_col).astype(BF), 'row', axis=0, tiled=True)  15.2 us
    unnamed x14, local copies, waits for them, and re-layouts  9.22 us
    psum x1, blocking collectives, on_device(): total = lax.psum(jnp.sum(m.astype(F32) ** 2), 'row')  6.25 us
    all_gather x1, waiting for transfers between devices, on_device(): panel = lax.all_gather(hamiltonian, 'col', axis=1, tiled=True)  5 us
  transfers between devices with their start and end apart: 6, of which 6 were waited for; matrix products, arithmetic and copies ran while one was open for 3% of the time, Pallas kernels for 0%

profile of v1, /device:TPU:0, one launch (start us, length us, event | category | flops | bytes accessed | tf_op | source)
XLA Modules:
  0.0 214.7 jit_solution(2861606941111251633)
XLA Ops:
  6.5 0.0 all-gather.11.cloned.1.call-start
  6.5 0.7 all-gather.11.cloned.1.call-update
  7.3 0.0 all-gather.7.cloned.1.call-start
  7.3 0.7 convert_bitcast_fusion
  8.0 75.1 %all-gather.2 = bf16[32,56,28]{1,2,0:T(8,128)(2,1)S(1)} all-gather(bf16[1,56,28]{1,2,0:T(8,128)(2,1)S(1)} %convert_bitcast_fusion), channel_id=2, replica_groups=mesh['row'=4,'col'=8] {'row','col'}, dimensions={0}, use_global_device_ids=true | all-gather | bytes 103488 | tf_op jit(solution)/shard_map/all_gather | solution.py:29
  83.2 0.2 copy.12
  83.3 0.2 reshape.30
  83.5 0.8 iota_subtract_fusion
  84.3 0.1 select_reduce_fusion.1
  84.4 0.9 convolution_convert_fusion.5
  85.3 0.9 convolution_convert_fusion.4
  86.2 5.0 %all-gather.11.cloned.1.call-done = bf16[8,364,728]{1,2,0:T(8,128)(2,1)} async-done(((bf16[1,364,728]{1,2,0:T(8,128)(2,1)}), bf16[8,364,728]{1,2,0:T(8,128)(2,1)}) %all-gather.11.cloned.1.call-update) | async-done | bytes 4239888 | tf_op jit(solution)/shard_map/all_gather | solution.py:28
  91.2 4.9 %copy.9 = bf16[8,364,728]{1,0,2:T(8,128)(2,1)} copy(bf16[8,364,728]{1,2,0:T(8,128)(2,1)} %all-gather.11.cloned.1.call-done) | data formatting | bytes 8479744 | tf_op jit(solution)/shard_map/all_gather | solution.py:28
  96.1 8.6 %reshape.34 = bf16[2912,728]{0,1:T(8,128)(2,1)} reshape(bf16[8,364,728]{1,0,2:T(8,128)(2,1)} %copy.9) | data formatting | bytes 8479744
  104.7 6.9 %multiply_reduce_fusion = (f32[]{:T(128)}, bf16[728,2912]{1,0:T(8,128)(2,1)}) fusion(s32[224]{0:T(256)S(1)} %get-tuple-element.8, s32[224]{0:T(256)S(1)} %get-tuple-element.7, bf16[56,224]{1,0:T(8,128)(2,1)S(1)} %convolution_convert_fusion.4, s32[56]{0:T(128)S(1)} %get-tuple-element.10, s32[56]{0:T(128)S(1)} %get-tuple-element.9, bf16[2912,728]{0,1:T(8,128)(2,1)} %reshape.34), kind=kOutput, calls=%fused_computation | convolution fusion | flops 987197120 | bytes 8507076 | tf_op jit(solution)/shard_map/dot_general | solution.py:12
  111.6 5.5 %fusion.26 = bf16[728,364]{1,0:T(8,128)(2,1)} fusion(bf16[728,2912]{1,0:T(8,128)(2,1)} %get-tuple-element.6, s32[364]{0:T(512)S(1)} %iota_add_fusion.1), kind=kOutput, calls=%fused_computation.30 | convolution fusion | flops 1544638336 | bytes 4771312 | tf_op jit(solution)/shard_map/dot_general | solution.py:12
  117.1 0.0 all-gather.7.cloned.1.call-update
  117.1 0.0 all-gather.9.cloned.1.call-start
  117.2 6.2 %psum.7 = f32[]{:T(128)} all-reduce(f32[]{:T(128)} %get-tuple-element.5), channel_id=1, replica_groups=mesh['row'=4,'col'=8] {'row'}, use_global_device_ids=true, to_apply=%region_3.4 | all-reduce | flops 1 | bytes 8 | tf_op jit(solution)/shard_map/psum | solution.py:44
  124.2 15.2 %all-gather.7.cloned.1.call-done = bf16[2912,364]{1,0:T(8,128)(2,1)} async-done(((bf16[728,364]{1,0:T(8,128)(2,1)}), bf16[2912,364]{1,0:T(8,128)(2,1)}) %all-gather.7.cloned.1.call-update) | async-done | bytes 2119952 | tf_op jit(solution)/shard_map/all_gather | solution.py:57
  139.3 5.4 %convolution_multiply_fusion = f32[728,364]{1,0:T(8,128)S(1)} fusion(bf16[728,2912]{1,0:T(8,128)(2,1)} %get-tuple-element.6, bf16[2912,364]{1,0:T(8,128)(2,1)} %all-gather.7.cloned.1.call-done, f32[]{:T(128)S(6)} %mul.107), kind=kOutput, calls=%fused_computation.18 | convolution fusion | flops 1543578368 | bytes 7419780 | tf_op jit(solution)/shard_map/dot_general | solution.py:12
  144.7 0.7 fusion.22
  145.4 0.3 collective-permute-start
  145.7 8.8 %collective-permute-done = bf16[728,364]{1,0:T(8,128)(2,1)S(1)} collective-permute-done((bf16[728,364]{1,0:T(8,128)(2,1)S(1)}, bf16[728,364]{1,0:T(8,128)(2,1)S(1)}, u32[]{:S(2)}, u32[]{:S(2)}) %collective-permute-start) | collective-permute-done | bytes 530016 | tf_op jit(solution)/shard_map/ppermute | solution.py:66
  154.4 0.0 collective-permute-start.1
  154.4 9.0 %collective-permute-done.1 = bf16[728,364]{1,0:T(8,128)(2,1)S(1)} collective-permute-done((bf16[728,364]{1,0:T(8,128)(2,1)S(1)}, bf16[728,364]{1,0:T(8,128)(2,1)S(1)}, u32[]{:S(2)}, u32[]{:S(2)}) %collective-permute-start.1) | collective-permute-done | bytes 530016 | tf_op jit(solution)/shard_map/ppermute | solution.py:66
  163.4 0.0 collective-permute-start.2
  163.4 9.0 %collective-permute-done.2 = bf16[728,364]{1,0:T(8,128)(2,1)S(1)} collective-permute-done((bf16[728,364]{1,0:T(8,128)(2,1)S(1)}, bf16[728,364]{1,0:T(8,128)(2,1)S(1)}, u32[]{:S(2)}, u32[]{:S(2)}) %collective-permute-start.2) | collective-permute-done | bytes 530016 | tf_op jit(solution)/shard_map/ppermute | solution.py:66
  172.4 0.1 constant_dynamic-update-slice_fusion.7
  172.4 0.1 constant_dynamic-update-slice_fusion.6
  172.5 0.1 constant_dynamic-update-slice_fusion.5
  172.6 0.1 constant_dynamic-update-slice_fusion.4
  172.7 0.1 constant_dynamic-update-slice_fusion.3
  172.8 0.1 constant_dynamic-update-slice_fusion.2
  172.9 0.1 constant_dynamic-update-slice_fusion.1
  173.0 0.1 constant_dynamic-update-slice_fusion
  173.1 0.0 copy-start.1
  173.1 0.0 copy-start.2
  173.2 5.7 %fusion.23 = bf16[728,364]{1,0:T(8,128)(2,1)} fusion(bf16[728,2912]{1,0:T(8,128)(2,1)} %get-tuple-element.6, bf16[5824,364]{1,0:T(8,128)(2,1)S(1)} %constant_dynamic-update-slice_fusion, s32[]{:T(128)S(6)} %select_n.33, f32[]{:T(128)S(6)} %rsqrt.3), kind=kOutput, calls=%fused_computation.29 | convolution fusion | flops 1543843328 | bytes 7006280 | tf_op jit(solution)/shard_map/dot_general | solution.py:12
  178.8 0.0 all-gather.9.cloned.1.call-update
  178.9 0.0 copy-done.1
  178.9 0.1 iota_subtract_fusion.1
  179.0 0.1 select_reduce_fusion
  179.1 0.0 copy-done.2
  179.1 2.5 %fusion.21 = f32[728,364]{1,0:T(8,128)S(1)} fusion(bf16[2912,364]{1,0:T(8,128)(2,1)S(1)} %copy-done.2, s32[728]{0:T(1024)S(1)} %iota_add_fusion, f32[]{:T(128)S(6)} %rsqrt.3), kind=kOutput, calls=%fused_computation.27 | convolution fusion | flops 1546493184 | bytes 3182820 | tf_op jit(solution)/shard_map/dot_general | solution.py:12
  181.6 0.0 copy-start
  181.6 20.7 %all-gather.9.cloned.1.call-done = bf16[2912,364]{1,0:T(8,128)(2,1)} async-done(((bf16[728,364]{1,0:T(8,128)(2,1)}), bf16[2912,364]{1,0:T(8,128)(2,1)}) %all-gather.9.cloned.1.call-update) | async-done | bytes 2119952 | tf_op jit(solution)/shard_map/all_gather | solution.py:70
  202.4 4.1 %fusion.18 = f32[728,364]{1,0:T(8,128)S(1)} fusion(f32[728,364]{1,0:T(8,128)S(1)} %fusion.21, bf16[2912,364]{1,0:T(8,128)(2,1)} %all-gather.9.cloned.1.call-done, s32[728]{0:T(1024)S(1)} %iota_add_fusion), kind=kOutput, calls=%fused_computation.24 | convolution fusion | flops 1545963264 | bytes 4242784 | tf_op jit(solution)/shard_map/dot_general | solution.py:12
  206.5 0.0 copy-done
  206.5 1.6 convolution_multiply_fusion.2
  (6 shorter events, 0.0 us)
Async XLA Ops:
  6.5 84.7 %all-gather.11.cloned.1.call-start = ((), (), s32[]{:S(2)}) async-start(), calls=%async_computation.2 | async-start | bytes 5031936 | tf_op jit(solution)/shard_map/all_gather | solution.py:28
  7.3 132.1 %all-gather.7.cloned.1.call-start = ((), (), s32[]{:S(2)}) async-start(), calls=%async_computation | async-start | bytes 2795520 | tf_op jit(solution)/shard_map/all_gather | solution.py:57
  117.1 85.3 %all-gather.9.cloned.1.call-start = ((), (), s32[]{:S(2)}) async-start(), calls=%async_computation.1 | async-start | bytes 2795520 | tf_op jit(solution)/shard_map/all_gather | solution.py:70
  145.4 9.0 %collective-permute-start = (bf16[728,364]{1,0:T(8,128)(2,1)S(1)}, bf16[728,364]{1,0:T(8,128)(2,1)S(1)}, u32[]{:S(2)}, u32[]{:S(2)}) collective-permute-start(bf16[728,364]{1,0:T(8,128)(2,1)S(1)} %fusion.22), channel_id=1, source_target_pairs={{0,8},{8,16},{16,24},{24,0},{1,9},{9,17},{17,25},{25,1},{2,10},{10... | collective-permute-start | bytes 1589960 | tf_op jit(solution)/shard_map/ppermute | solution.py:66
  154.4 9.0 %collective-permute-start.1 = (bf16[728,364]{1,0:T(8,128)(2,1)S(1)}, bf16[728,364]{1,0:T(8,128)(2,1)S(1)}, u32[]{:S(2)}, u32[]{:S(2)}) collective-permute-start(bf16[728,364]{1,0:T(8,128)(2,1)S(1)} %collective-permute-done), channel_id=1, source_target_pairs={{0,8},{8,16},{16,24},{24,0},{1,9},{9,17},{17,25},{25,1},{2,10},{10... | collective-permute-start | bytes 1589960 | tf_op jit(solution)/shard_map/ppermute | solution.py:66
  163.4 9.0 %collective-permute-start.2 = (bf16[728,364]{1,0:T(8,128)(2,1)S(1)}, bf16[728,364]{1,0:T(8,128)(2,1)S(1)}, u32[]{:S(2)}, u32[]{:S(2)}) collective-permute-start(bf16[728,364]{1,0:T(8,128)(2,1)S(1)} %collective-permute-done.1), channel_id=1, source_target_pairs={{0,8},{8,16},{16,24},{24,0},{1,9},{9,17},{17,25},{25,1},{2,10},{10... | collective-permute-start | bytes 1589960 | tf_op jit(solution)/shard_map/ppermute | solution.py:66
  173.1 5.7 %copy-start.1 = (s32[224]{0:T(256)S(1)}, s32[224]{0:T(256)}, u32[]{:S(2)}) copy-start(s32[224]{0:T(256)} %param.4) | copy-start | bytes 2692
  173.1 5.9 %copy-start.2 = (bf16[2912,364]{1,0:T(8,128)(2,1)S(1)}, bf16[2912,364]{1,0:T(8,128)(2,1)}, u32[]{:S(2)}) copy-start(bf16[2912,364]{1,0:T(8,128)(2,1)} %all-gather.7.cloned.1.call-done) | copy-start | bytes 6359812
  181.6 24.9 %copy-start = (s32[56,28]{0,1:T(8,128)S(1)}, s32[56,28]{0,1:T(8,128)}, u32[]{:S(2)}) copy-start(s32[56,28]{0,1:T(8,128)} %param.5) | copy-start | bytes 18820
Sparse Core Ops, SparseCore 0:
  9.5 81.6 all-gather.10
  117.2 22.0 all-gather.6
  179.0 23.3 all-gather.8
